TPU v7x, 32 devices: a whole 2x2x4 slice. The times are simulated.
32 devices in a mesh: gx: 8 (over y, x, core), gy: 4 (over z).
Axes of the slice: x: 2, y: 2, z: 4, core: 2. Of those that a mesh axis runs over, the one named last changes fastest.
Arguments:
- fields: float32 [8, 2048, 2048], P(None, 'gx', 'gy'), may hold values from -6 to 6
- wave_order: int32 [1024], replicated, may hold values from 0 to 1023, as said below
- kept_mask: int32 [1024, 2048], P('gx', 'gy'), may hold values from 0 to 1, as said below
Outputs:
- spectral: float32 [2, 8, 1024, 2048], P(None, None, 'gx', 'gy')
Inputs may be any that keep to these rules, and one draw needn't show every extreme that they name: `wave_order`: each x-wavenumber 0 to 1023 once. `kept_mask`: in each row the kept y-wavenumbers q are those with min(q, 2048 - q) up to a bound that does not grow with the row's x-wavenumber.
All inputs are finite; a program needn't handle non-finite values.
Results may differ from a plain program's by a relative error of at most 0.00007.
Values sent between devices are 32-bit elements; how exact they have to be, the bound alone decides.
A program may use at most 192 MiB of HBM per device.

v0:
```python
import functools
import math

import jax
import jax.numpy as jnp
import numpy as np
from jax import lax
from jax.experimental import pallas as pl
from jax.experimental.pallas import tpu as pltpu
from jax.sharding import PartitionSpec as P

NX = 2048
NY = 2048
STACK = 8
KX = 1024


def wave_angles(wave_ids, points, period):
    phases = wave_ids[:, None] * points[None, :] % period
    angles = phases.astype(jnp.float32) * (2.0 * math.pi / period)
    return (jnp.cos(angles), jnp.sin(angles))


def x_terms(cos_table, sin_table, values):
    stack_count, x_count, y_count = values.shape
    waves = cos_table.shape[0]
    table = jnp.concatenate([cos_table, -sin_table], axis=0)
    flat = jnp.transpose(values, (1, 0, 2)).reshape(x_count, stack_count * y_count)
    product = jnp.dot(
        table, flat, precision=lax.Precision.HIGHEST, preferred_element_type=jnp.float32
    )
    product = product.reshape(2, waves, stack_count, y_count)
    return jnp.transpose(product, (1, 0, 2, 3))


def y_terms(cos_table, sin_table, spectra):
    rows, parts, stack_count, y_count = spectra.shape
    waves = cos_table.shape[0]
    table = jnp.concatenate([cos_table, sin_table], axis=0)
    flat = spectra.reshape(rows * parts * stack_count, y_count)
    product = jnp.dot(
        flat, table.T, precision=lax.Precision.HIGHEST, preferred_element_type=jnp.float32
    )
    product = product.reshape(rows, parts, stack_count, 2, waves)
    real_part = product[:, 0, :, 0] + product[:, 1, :, 1]
    imag_part = product[:, 1, :, 0] - product[:, 0, :, 1]
    return jnp.stack([real_part, imag_part], axis=1)


def shards(fields, wave_order, kept_mask):
    x_every = jnp.arange(NX, dtype=jnp.int32)
    x_cos, x_sin = wave_angles(wave_order, x_every, NX)
    partial_terms = x_terms(
        x_cos, x_sin, lax.all_to_all(fields, "gx", split_axis=2, concat_axis=1, tiled=True)
    )
    spectra = lax.all_to_all(partial_terms, "gx", split_axis=0, concat_axis=3, tiled=True)
    y_every = jnp.arange(NY, dtype=jnp.int32)
    y_cos, y_sin = wave_angles(y_every, y_every, NY)
    y_spectra = y_terms(
        y_cos, y_sin, lax.all_to_all(spectra, "gy", split_axis=0, concat_axis=3, tiled=True)
    )
    result = lax.all_to_all(y_spectra, "gy", split_axis=3, concat_axis=0, tiled=True)
    weight = kept_mask.astype(jnp.float32) * (1.0 / math.sqrt(NX * NY))
    arranged = jnp.transpose(result, (1, 2, 0, 3)) * weight[None, None]
    return arranged


LANES = 128
MESH_IDS = pl.DeviceIdType.MESH


def split_halves(values):
    high = values.astype(jnp.bfloat16)
    return high, (values - high.astype(jnp.float32)).astype(jnp.bfloat16)


def table_halves(table):
    high = table.astype(jnp.bfloat16)
    low = (table - high.astype(np.float64)).astype(jnp.bfloat16)
    return jnp.asarray(high), jnp.asarray(low)


def mxu(left, right):
    return jnp.dot(left, right, preferred_element_type=jnp.float32)


def y_tables(y_local, parts):
    points = np.arange(y_local)
    period = y_local * parts
    turns = np.arange(parts)[:, None] * points[None, :] % period * (2.0 * np.pi / period)
    twiddle = jnp.asarray(np.concatenate([np.cos(turns), np.sin(turns)]), jnp.float32)
    angles = points[:, None] * points[None, :] % y_local * (2.0 * np.pi / y_local)
    cos = np.cos(angles).reshape(y_local, parts, -1)
    sin = np.sin(angles).reshape(y_local, parts, -1)
    both = np.concatenate([cos, sin], axis=2).transpose(1, 0, 2)
    high, low = table_halves(both)
    wide = y_local // parts
    order = np.zeros((y_local, y_local), np.float32)
    for residue in range(parts):
        order[residue * wide + np.arange(wide), parts * np.arange(wide) + residue] = 1.0
    return twiddle, high, low, jnp.asarray(order, jnp.bfloat16)


def exchange_kernel(
    gx, gy, levels, chunks,
    fields, order_column, twiddle, y_high_in, y_low_in, order_in, out,
    x_high, x_low, lines, split_lines, waves, held, columns, z_high, z_low, spectra,
    y_high, y_low, order, whole_y,
    send_r, recv_r, send_a, recv_a, send_b, recv_b, send_c, recv_c, send_d, recv_d, table_sem,
):
    me = lax.axis_index("gx")
    my = lax.axis_index("gy")
    x_local = fields.shape[1]
    y_local = fields.shape[2]
    rows = out.shape[3]
    first = chunks // 2
    cuts = y_local // LANES
    block = 2 * rows * gy
    nx = gx * x_local
    near = gy // 2
    far_half = (1 - my // near) * near
    near_half = my // near * near
    x_order = (6, 7, 4, 2, 5, 3, 1, 0)
    y_order = (3, 2, 1, 0)

    def partner(index, o):
        total = 0
        for bit in (1, 2, 4):
            total = total + bit * lax.rem(index // bit + o // bit, 2)
        return total

    def move(axis, target, src, dst, send, recv):
        def remote():
            return pltpu.make_async_remote_copy(
                src_ref=src, dst_ref=dst, send_sem=send, recv_sem=recv,
                device_id={axis: target}, device_id_type=MESH_IDS,
            )

        def local():
            return pltpu.make_async_copy(src, dst, recv)

        return remote, local

    def copy_r(c, o):
        to = partner(my, o)
        return move(
            "gy", to, fields.at[first * levels + to], whole_y.at[my],
            send_r.at[c, o], recv_r.at[c, o],
        )

    def copy_a(c, o):
        to = partner(me, o)
        level = c % first * levels + to // cuts
        source = fields if c < first else whole_y
        lane = pl.multiple_of(lax.rem(to, cuts) * LANES, LANES)
        return move(
            "gx", to,
            source.at[level, :, pl.ds(lane, LANES)],
            lines.at[c, pl.ds(pl.multiple_of(me * x_local, x_local), x_local), :],
            send_a.at[c, o], recv_a.at[c, o],
        )

    def copy_b(c, o, late):
        to = partner(me, o)
        lane = pl.multiple_of(lax.rem(me, cuts) * LANES, LANES)
        start = near_half if late else far_half
        half = pl.ds(start, near)
        if c < first:
            landing = held.at[c, half, me // cuts, :, pl.ds(lane, LANES)]
        else:
            piece = c % first * levels + me // cuts
            landing = columns.at[first + start // near, piece, :, :, pl.ds(lane, LANES)]
        return move(
            "gx", to,
            waves.at[c, o, half],
            landing,
            send_b.at[late, c, o], recv_b.at[late, c, o],
        )

    def copy_c(c, o):
        to = partner(my, o)
        return move(
            "gy", to, held.at[c, to], columns.at[c, my], send_c.at[c, o], recv_c.at[c, o]
        )

    def copy_d(c, o):
        to = partner(my, o)
        if c < first:
            landing = out.at[:, pl.ds(c * levels, levels), my]
        else:
            landing = out.at[:, first * levels + my, pl.ds(c % first * levels, levels)]
        return move(
            "gy", to,
            spectra.at[c, o],
            landing,
            send_d.at[c, o], recv_d.at[c, o],
        )

    def start_all(copy, c, offsets):
        for o in offsets:
            remote, local = copy(c, o)
            (remote() if o else local()).start()

    def arrive(copy, c, offsets):
        for o in offsets:
            remote, local = copy(c, o)
            if o:
                remote().wait_recv()
            else:
                local().wait()

    def first_b(c, o):
        return copy_b(c, o, 0)

    def late_b(c, o):
        return copy_b(c, o, 1)

    def circle(phases):
        turns = phases.astype(jnp.float32) * (1.0 / nx)
        halves = jnp.floor(2.0 * turns + 0.5)
        angle = (turns - 0.5 * halves) * (2.0 * math.pi)
        sign = 1.0 - 2.0 * halves * (2.0 - halves)
        square = angle * angle
        cos = jnp.full_like(square, 1.0 / math.factorial(12))
        sin = jnp.full_like(square, 1.0 / math.factorial(13))
        for power in range(10, -1, -2):
            flip = -1.0 if power % 4 else 1.0
            cos = cos * square + flip / math.factorial(power)
            sin = sin * square + flip / math.factorial(power + 1)
        return cos * sign, sin * angle * sign

    def make_table(step, carry):
        waves_at = order_column[pl.ds(pl.multiple_of(step * rows, rows), rows), :]
        points = lax.broadcasted_iota(jnp.int32, (rows, x_local), 1)
        near_cos, near_sin = circle(waves_at * points & (nx - 1))
        blocks = lax.broadcasted_iota(jnp.int32, (rows, LANES), 1) * x_local
        far_cos, far_sin = circle(waves_at * blocks & (nx - 1))
        first = pl.multiple_of(2 * step * rows, rows)
        for j in range(gx):
            cos, sin = far_cos[:, j : j + 1], far_sin[:, j : j + 1]
            lanes = slice(j * x_local, (j + 1) * x_local)
            for part, value in enumerate(
                (cos * near_cos - sin * near_sin, -(sin * near_cos + cos * near_sin))
            ):
                at = pl.ds(pl.multiple_of(first + part * rows, rows), rows)
                high, low = split_halves(value)
                x_high[at, lanes] = high
                x_low[at, lanes] = low
        return carry

    def x_stage(c):
        def split_block(j, carry):
            at = pl.ds(pl.multiple_of(j * x_local, x_local), x_local)
            high, low = split_halves(lines[c, at, :])
            split_lines[at, :LANES] = high
            split_lines[at, LANES:] = low
            return carry

        lax.fori_loop(0, gx, split_block, 0)

        def one(step, carry):
            o = gx - 1 - step
            to = partner(me, o)
            at = pl.ds(pl.multiple_of(to * block, block), block)
            main = mxu(x_high[at, :], split_lines[...])
            rest = mxu(x_low[at, :], split_lines[:, :LANES])
            total = main[:, :LANES] + main[:, LANES:] + rest
            waves[c, o] = total.reshape(gy, 2 * rows, LANES)
            remote, local = first_b(c, o)
            pl.when(o != 0)(lambda: remote().start())
            pl.when(o == 0)(lambda: local().start())
            return carry

        lax.fori_loop(0, gx, one, 0)
        start_all(late_b, c, x_order)

    def y_stage(c):
        size = 16
        span = levels * rows
        for level in range(levels):
            for i in range(0, rows, size):
                re = [columns[c, g, level, i : i + size, :] for g in range(4)]
                im = [columns[c, g, level, rows + i : rows + i + size, :] for g in range(4)]
                re_even, re_odd = re[0] + re[2], re[0] - re[2]
                im_even, im_odd = im[0] + im[2], im[0] - im[2]
                re_sum, re_gap = re[1] + re[3], re[1] - re[3]
                im_sum, im_gap = im[1] + im[3], im[1] - im[3]
                legs = (
                    (re_even + re_sum, im_even + im_sum),
                    (re_odd + im_gap, im_odd - re_gap),
                    (re_even - re_sum, im_even - im_sum),
                    (re_odd - im_gap, im_odd + re_gap),
                )
                for r, (a, b) in enumerate(legs):
                    cos = twiddle[r : r + 1, :]
                    sin = twiddle[gy + r : gy + r + 1, :]
                    for part, value in enumerate((a * cos + b * sin, b * cos - a * sin)):
                        at = part * gy * span + r * span + level * rows + i
                        high, low = split_halves(value)
                        z_high[at : at + size, :] = high
                        z_low[at : at + size, :] = low

        def one(step, carry):
            o = gy - 1 - step
            to = partner(my, o)
            table = y_high[to]
            terms = mxu(z_high[...], table) + mxu(z_low[...], table) + mxu(z_high[...], y_low[to])
            half = gy * span
            wide = y_local // gy
            re = terms[:half, :wide] + terms[half:, wide:]
            im = terms[half:, :wide] - terms[:half, wide:]
            whole = jnp.concatenate(
                [
                    jnp.concatenate([piece[r * span : (r + 1) * span] for r in range(gy)], axis=1)
                    for piece in (re, im)
                ],
                axis=0,
            )
            high, low = split_halves(whole)
            ordered = mxu(high, order[...]) + mxu(low, order[...])
            spectra[c, o] = ordered.reshape(2, levels, rows, y_local)
            remote, local = copy_d(c, o)
            pl.when(o != 0)(lambda: remote().start())
            pl.when(o == 0)(lambda: local().start())
            return carry

        lax.fori_loop(0, gy, one, 0)

    start_all(copy_r, 0, y_order)
    start_all(copy_a, 0, x_order)
    tables = [
        pltpu.make_async_copy(src, dst, table_sem.at[i])
        for i, (src, dst) in enumerate(
            ((y_high_in, y_high), (y_low_in, y_low), (order_in, order))
        )
    ]
    for table in tables:
        table.start()
    lax.fori_loop(0, x_high.shape[0] // (2 * rows), make_table, 0)
    for table in tables:
        table.wait()

    def forward(c):
        arrive(first_b, c, x_order)
        start_all(copy_c, c, (3, 2))
        arrive(late_b, c, x_order)
        start_all(copy_c, c, (1, 0))

    def lines_stage(c):
        arrive(copy_a, c, x_order)
        x_stage(c)

    def columns_stage(c):
        arrive(copy_c, c, y_order)
        y_stage(c)

    lines_stage(0)
    start_all(copy_a, 1, x_order)
    forward(0)
    lines_stage(1)
    arrive(copy_r, 0, y_order)
    start_all(copy_a, 2, x_order)
    start_all(copy_a, 3, x_order)
    forward(1)
    columns_stage(0)
    lines_stage(2)
    lines_stage(3)
    columns_stage(1)
    for c in (2, 3):
        arrive(first_b, c, x_order)
        arrive(late_b, c, x_order)
    y_stage(2)
    y_stage(3)

    def sent(copy, c, offsets):
        for o in offsets:
            if o:
                copy(c, o)[0]().wait_send()

    for c in range(chunks):
        arrive(copy_d, c, y_order)
    sent(copy_r, 0, y_order)
    for c in range(chunks):
        for copy in (copy_a, first_b, late_b):
            sent(copy, c, x_order)
        if c < first:
            sent(copy_c, c, y_order)
        sent(copy_d, c, y_order)


def kernel_shards(gx, gy, fields, wave_order, kept_mask):
    stack, x_local, y_local = fields.shape
    nx, ny = x_local * gx, y_local * gy
    levels = gx * LANES // y_local
    chunks = stack // levels
    rows = wave_order.shape[0] // (gx * gy)
    all_rows = 2 * wave_order.shape[0]
    twiddle, y_high, y_low, order = y_tables(y_local, gy)
    vmem = pl.BlockSpec(memory_space=pltpu.VMEM)
    hbm = pl.BlockSpec(memory_space=pl.ANY)
    z_rows = 2 * gy * levels * rows
    spectra = pl.pallas_call(
        functools.partial(exchange_kernel, gx, gy, levels, chunks),
        out_shape=jax.ShapeDtypeStruct((2, stack, gy, rows, y_local), jnp.float32),
        in_specs=[hbm, vmem, vmem] + [hbm] * 3,
        out_specs=hbm,
        scratch_shapes=[
            pltpu.VMEM((all_rows, nx), jnp.bfloat16),
            pltpu.VMEM((all_rows, nx), jnp.bfloat16),
            pltpu.VMEM((chunks, nx, LANES), jnp.float32),
            pltpu.VMEM((nx, 2 * LANES), jnp.bfloat16),
            pltpu.VMEM((chunks, gx, gy, 2 * rows, LANES), jnp.float32),
            pltpu.VMEM((chunks, gy, levels, 2 * rows, y_local), jnp.float32),
            pltpu.VMEM((chunks, gy, levels, 2 * rows, y_local), jnp.float32),
            pltpu.VMEM((z_rows, y_local), jnp.bfloat16),
            pltpu.VMEM((z_rows, y_local), jnp.bfloat16),
            pltpu.VMEM((chunks, gy, 2, levels, rows, y_local), jnp.float32),
            pltpu.VMEM(y_high.shape, jnp.bfloat16),
            pltpu.VMEM(y_low.shape, jnp.bfloat16),
            pltpu.VMEM(order.shape, jnp.bfloat16),
            pltpu.VMEM((gy, x_local, y_local), jnp.float32),
        ]
        + [pltpu.SemaphoreType.DMA((1, gy))] * 2
        + [pltpu.SemaphoreType.DMA((chunks, gx))] * 2
        + [pltpu.SemaphoreType.DMA((2, chunks, gx))] * 2
        + [pltpu.SemaphoreType.DMA((chunks, gy))] * 4
        + [pltpu.SemaphoreType.DMA((3,))],
        compiler_params=pltpu.CompilerParams(
            has_side_effects=True, vmem_limit_bytes=62 * 1024 * 1024
        ),
        name="exchange",
    )(fields, wave_order[:, None], twiddle, y_high, y_low, order)
    weight = kept_mask.astype(jnp.float32) * (1.0 / math.sqrt(nx * ny))
    return spectra.reshape(2, stack, gy * rows, y_local) * weight[None, None]


def kernel_fits(gx, gy):
    y_local, x_local = NY // gy, NX // gx
    if gx != 8 or gy != 4 or NX & (NX - 1) or y_local % (4 * LANES) or x_local % LANES or gx * LANES % y_local:
        return False
    levels = gx * LANES // y_local
    return STACK == 4 * levels == 2 * gy and KX % (gx * gy * 16) == 0


def solution(mesh):
    gx, gy = mesh.shape["gx"], mesh.shape["gy"]
    body = functools.partial(kernel_shards, gx, gy) if kernel_fits(gx, gy) else shards
    return jax.shard_map(
        body,
        mesh=mesh,
        in_specs=(P(None, "gx", "gy"), P(), P("gx", "gy")),
        out_specs=P(None, None, "gx", "gy"),
        check_vma=False,
    )
```

profile of v0, /device:TPU:0, one launch (start us, length us, event | category | flops | bytes accessed | tf_op | source)
XLA Modules:
  0.0 202.1 jit_solution(13200478660114399621)
XLA Ops:
  0.0 1.0 convert_multiply_fusion
  1.0 1.7 copy.8.order_column
  2.7 194.6 %exchange.1 = f32[2,8,4,32,512]{4,3,2,1,0:T(8,128)} custom-call(f32[8,256,512]{2,1,0:T(8,128)} %fields.1, s32[1024,1]{1,0:T(8,128)} %copy.8.order_column, f32[8,512]{1,0:T(8,128)} %constant.10.clone.twiddle, bf16[4,512,256]{2,1,0:T(8,128)(2,1)} %constant.11.clone.y_high_in, bf16[4,512,256]{2,1,0:T(8,128)(2,1)} %constant.12.clone.y_low_in, ...), custom_call_target="tpu_custom_call" | custom-call | tf_op jit(solution)/shard_map/exchange/pallas_call | solution.py:402
  197.3 4.8 %bitcast_multiply_fusion = f32[2,8,128,512]{3,2,1,0:T(8,128)} fusion(f32[2,8,4,32,512]{4,3,2,1,0:T(8,128)} %exchange.1, f32[128,512]{1,0:T(8,128)S(1)} %convert_multiply_fusion), kind=kLoop, calls=%fused_computation | loop fusion | flops 1048576 | bytes 8650752 | tf_op jit(solution)/shard_map/mul | solution.py:434
where the time goes:
time: 202 us
  Pallas kernels  195 us (97%)
  other arithmetic  5.76 us (3%)
    pallas_call x1, Pallas kernels, kernel_shards(): pl.pallas_call(functools.partial(exchange_kernel, gx, gy, levels, chunks)...  195 us
    mul x1, other arithmetic, kernel_shards(): return spectra.reshape(2, stack, gy * rows, y_local) * weight[None, None]  4.79 us

commit v1 on v0

--- a/solution.py
+++ b/solution.py
@@ -103,8 +103,8 @@
 
 def exchange_kernel(
     gx, gy, levels, chunks,
-    fields, order_column, twiddle, y_high_in, y_low_in, order_in, out,
-    x_high, x_low, lines, split_lines, waves, held, columns, z_high, z_low, spectra,
+    fields, order_rows, twiddle, y_high_in, y_low_in, order_in, out,
+    order_column, x_high, x_low, lines, split_lines, waves, held, columns, z_high, z_low, spectra,
     y_high, y_low, order, whole_y,
     send_r, recv_r, send_a, recv_a, send_b, recv_b, send_c, recv_c, send_d, recv_d, table_sem,
 ):
@@ -232,7 +232,8 @@
     def make_table(step, carry):
         waves_at = order_column[pl.ds(pl.multiple_of(step * rows, rows), rows), :]
         points = lax.broadcasted_iota(jnp.int32, (rows, x_local), 1)
-        near_cos, near_sin = circle(waves_at * points & (nx - 1))
+        near_waves = jnp.concatenate([waves_at] * (x_local // LANES), axis=1)
+        near_cos, near_sin = circle(near_waves * points & (nx - 1))
         blocks = lax.broadcasted_iota(jnp.int32, (rows, LANES), 1) * x_local
         far_cos, far_sin = circle(waves_at * blocks & (nx - 1))
         first = pl.multiple_of(2 * step * rows, rows)
@@ -326,6 +327,14 @@
 
         lax.fori_loop(0, gy, one, 0)
 
+    barrier = pltpu.get_barrier_semaphore()
+    for axis, index, size in (("gy", my, gy), ("gx", me, gx)):
+        for o in range(1, size):
+            pl.semaphore_signal(
+                barrier, inc=1, device_id={axis: partner(index, o)}, device_id_type=MESH_IDS
+            )
+    pl.semaphore_wait(barrier, gx + gy - 2)
+
     start_all(copy_r, 0, y_order)
     start_all(copy_a, 0, x_order)
     tables = [
@@ -336,6 +345,9 @@
     ]
     for table in tables:
         table.start()
+    for i in range(order_rows.shape[0]):
+        row = jnp.broadcast_to(order_rows[i : i + 1, :], (LANES, LANES))
+        order_column[i * LANES : (i + 1) * LANES, :] = row.T
     lax.fori_loop(0, x_high.shape[0] // (2 * rows), make_table, 0)
     for table in tables:
         table.wait()
@@ -388,6 +400,20 @@
         sent(copy_d, c, y_order)
 
 
+def keep_kernel(scale, spectra, kept_mask, out, kept, sems):
+    copies = []
+    for piece in range(spectra.shape[0]):
+        kept[piece] = spectra[piece] * (kept_mask[...].astype(jnp.float32) * scale)
+        copies.append(pltpu.make_async_copy(kept.at[piece], out.at[piece], sems.at[piece]))
+        copies[-1].start()
+    for copy in copies:
+        copy.wait()
+
+
+def stay(value):
+    return pltpu.with_memory_space_constraint(value, pltpu.HBM)
+
+
 def kernel_shards(gx, gy, fields, wave_order, kept_mask):
     stack, x_local, y_local = fields.shape
     nx, ny = x_local * gx, y_local * gy
@@ -397,14 +423,16 @@
     all_rows = 2 * wave_order.shape[0]
     twiddle, y_high, y_low, order = y_tables(y_local, gy)
     vmem = pl.BlockSpec(memory_space=pltpu.VMEM)
+    anywhere = pl.BlockSpec(memory_space=pl.ANY)
     hbm = pl.BlockSpec(memory_space=pl.ANY)
     z_rows = 2 * gy * levels * rows
     spectra = pl.pallas_call(
         functools.partial(exchange_kernel, gx, gy, levels, chunks),
-        out_shape=jax.ShapeDtypeStruct((2, stack, gy, rows, y_local), jnp.float32),
+        out_shape=pltpu.VMEM((2, stack, gy, rows, y_local), jnp.float32),
         in_specs=[hbm, vmem, vmem] + [hbm] * 3,
-        out_specs=hbm,
+        out_specs=anywhere,
         scratch_shapes=[
+            pltpu.VMEM((wave_order.shape[0], LANES), jnp.int32),
             pltpu.VMEM((all_rows, nx), jnp.bfloat16),
             pltpu.VMEM((all_rows, nx), jnp.bfloat16),
             pltpu.VMEM((chunks, nx, LANES), jnp.float32),
@@ -426,12 +454,24 @@
         + [pltpu.SemaphoreType.DMA((chunks, gy))] * 4
         + [pltpu.SemaphoreType.DMA((3,))],
         compiler_params=pltpu.CompilerParams(
-            has_side_effects=True, vmem_limit_bytes=62 * 1024 * 1024
+            collective_id=0, has_side_effects=True, vmem_limit_bytes=58 * 1024 * 1024
         ),
         name="exchange",
-    )(fields, wave_order[:, None], twiddle, y_high, y_low, order)
-    weight = kept_mask.astype(jnp.float32) * (1.0 / math.sqrt(nx * ny))
-    return spectra.reshape(2, stack, gy * rows, y_local) * weight[None, None]
+    )(stay(fields), wave_order.reshape(-1, LANES), twiddle, stay(y_high), stay(y_low), stay(order))
+    pieces = 2 * stack
+    kept = pl.pallas_call(
+        functools.partial(keep_kernel, 1.0 / math.sqrt(nx * ny)),
+        out_shape=jax.ShapeDtypeStruct((pieces, gy * rows, y_local), jnp.float32),
+        in_specs=[vmem, vmem],
+        out_specs=anywhere,
+        scratch_shapes=[
+            pltpu.VMEM((pieces, gy * rows, y_local), jnp.float32),
+            pltpu.SemaphoreType.DMA((pieces,)),
+        ],
+        compiler_params=pltpu.CompilerParams(vmem_limit_bytes=6 * 1024 * 1024),
+        name="keep",
+    )(spectra.reshape(pieces, gy * rows, y_local), kept_mask)
+    return kept.reshape(2, stack, gy * rows, y_local)
 
 
 def kernel_fits(gx, gy):

time: 202 us -> 193 us (0.955)
  other arithmetic: 5.76 us -> 0 us
    mul x2 -> x0, other arithmetic: 5.76 us -> none  [the longest x1 4.79 us: kernel_shards(): return spectra.reshape(2, stack, gy * rows, y_local) * weight[None, None]]
    pallas_call x1, Pallas kernels: 195 us -> 191 us  [kernel_shards(): pl.pallas_call(functools.partial(exchange_kernel, gx, gy, levels, chunks)...]
    pallas_call x0 -> x1, Pallas kernels: none -> 2.17 us  [kernel_shards(): pl.pallas_call(functools.partial(keep_kernel, 1.0 / math.sqrt(nx * ny)),...]
where the time goes in v1:
time: 193 us
  Pallas kernels  193 us (100%)
    pallas_call x1, Pallas kernels, kernel_shards(): pl.pallas_call(functools.partial(exchange_kernel, gx, gy, levels, chunks)...  191 us

profile of v1, /device:TPU:0, one launch (start us, length us, event | category | flops | bytes accessed | tf_op | source)
XLA Modules:
  0.0 193.1 jit_solution(4642709670404787568)
XLA Ops:
  0.0 0.0 copy-start
  0.0 190.9 %exchange.1 = f32[2,8,4,32,512]{4,3,2,1,0:T(8,128)S(1)} custom-call(f32[8,256,512]{2,1,0:T(8,128)} %fields.1, s32[8,128]{1,0:T(8,128)} %bitcast.4, f32[8,512]{1,0:T(8,128)} %constant.8.clone.twiddle, bf16[4,512,256]{2,1,0:T(8,128)(2,1)} %constant.9.clone.y_high_in, bf16[4,512,256]{2,1,0:T(8,128)(2,1)} %constant.10.clone.y_low_in, ...), custom_call_target="tpu_custom_call" | custom-call | tf_op jit(solution)/shard_map/exchange/pallas_call | solution.py:429
  190.9 0.0 copy-done
  190.9 2.2 %keep.1 = f32[16,128,512]{2,1,0:T(8,128)} custom-call(f32[16,128,512]{2,1,0:T(8,128)S(1)} %bitcast.3, s32[128,512]{1,0:T(8,128)S(1)} %copy-done), custom_call_target="tpu_custom_call" | custom-call | tf_op jit(solution)/shard_map/keep/pallas_call | solution.py:462
Async XLA Ops:
  0.0 190.9 %copy-start = (s32[128,512]{1,0:T(8,128)S(1)}, s32[128,512]{1,0:T(8,128)}, u32[]{:S(2)}) copy-start(s32[128,512]{1,0:T(8,128)} %kept_mask.1) | copy-start | bytes 786436

commit v2 on v1

--- a/solution.py
+++ b/solution.py
@@ -103,8 +103,8 @@
 
 def exchange_kernel(
     gx, gy, levels, chunks,
-    fields, order_rows, twiddle, y_high_in, y_low_in, order_in, out,
-    order_column, x_high, x_low, lines, split_lines, waves, held, columns, z_high, z_low, spectra,
+    fields, order_rows_in, twiddle_in, y_high_in, y_low_in, order_in, out,
+    order_rows, twiddle, order_column, x_high, x_low, lines, split_lines, waves, held, columns, z_high, z_low, spectra,
     y_high, y_low, order, whole_y,
     send_r, recv_r, send_a, recv_a, send_b, recv_b, send_c, recv_c, send_d, recv_d, table_sem,
 ):
@@ -128,6 +128,13 @@
         for bit in (1, 2, 4):
             total = total + bit * lax.rem(index // bit + o // bit, 2)
         return total
+
+    def turn(step):
+        inner = lax.rem(my + 1, gy) // 2
+        is_first = (3 - step) // 3
+        is_second = lax.rem(step, 2) * ((3 - step) // 2)
+        is_third = step // 2 * ((4 - step) // 2)
+        return is_first * (1 + inner) + is_second * 3 + is_third * (2 - inner)
 
     def move(axis, target, src, dst, send, recv):
         def remote():
@@ -302,7 +309,7 @@
                         z_low[at : at + size, :] = low
 
         def one(step, carry):
-            o = gy - 1 - step
+            o = turn(step)
             to = partner(my, o)
             table = y_high[to]
             terms = mxu(z_high[...], table) + mxu(z_low[...], table) + mxu(z_high[...], y_low[to])
@@ -340,16 +347,23 @@
     tables = [
         pltpu.make_async_copy(src, dst, table_sem.at[i])
         for i, (src, dst) in enumerate(
-            ((y_high_in, y_high), (y_low_in, y_low), (order_in, order))
+            (
+                (order_rows_in, order_rows),
+                (twiddle_in, twiddle),
+                (y_high_in, y_high),
+                (y_low_in, y_low),
+                (order_in, order),
+            )
         )
     ]
     for table in tables:
         table.start()
+    tables[0].wait()
     for i in range(order_rows.shape[0]):
         row = jnp.broadcast_to(order_rows[i : i + 1, :], (LANES, LANES))
         order_column[i * LANES : (i + 1) * LANES, :] = row.T
     lax.fori_loop(0, x_high.shape[0] // (2 * rows), make_table, 0)
-    for table in tables:
+    for table in tables[1:]:
         table.wait()
 
     def forward(c):
@@ -422,6 +436,7 @@
     rows = wave_order.shape[0] // (gx * gy)
     all_rows = 2 * wave_order.shape[0]
     twiddle, y_high, y_low, order = y_tables(y_local, gy)
+    order_rows = wave_order.reshape(-1, LANES)
     vmem = pl.BlockSpec(memory_space=pltpu.VMEM)
     anywhere = pl.BlockSpec(memory_space=pl.ANY)
     hbm = pl.BlockSpec(memory_space=pl.ANY)
@@ -429,9 +444,11 @@
     spectra = pl.pallas_call(
         functools.partial(exchange_kernel, gx, gy, levels, chunks),
         out_shape=pltpu.VMEM((2, stack, gy, rows, y_local), jnp.float32),
-        in_specs=[hbm, vmem, vmem] + [hbm] * 3,
+        in_specs=[hbm] * 6,
         out_specs=anywhere,
         scratch_shapes=[
+            pltpu.VMEM(order_rows.shape, jnp.int32),
+            pltpu.VMEM(twiddle.shape, jnp.float32),
             pltpu.VMEM((wave_order.shape[0], LANES), jnp.int32),
             pltpu.VMEM((all_rows, nx), jnp.bfloat16),
             pltpu.VMEM((all_rows, nx), jnp.bfloat16),
@@ -452,12 +469,12 @@
         + [pltpu.SemaphoreType.DMA((chunks, gx))] * 2
         + [pltpu.SemaphoreType.DMA((2, chunks, gx))] * 2
         + [pltpu.SemaphoreType.DMA((chunks, gy))] * 4
-        + [pltpu.SemaphoreType.DMA((3,))],
+        + [pltpu.SemaphoreType.DMA((5,))],
         compiler_params=pltpu.CompilerParams(
             collective_id=0, has_side_effects=True, vmem_limit_bytes=58 * 1024 * 1024
         ),
         name="exchange",
-    )(stay(fields), wave_order.reshape(-1, LANES), twiddle, stay(y_high), stay(y_low), stay(order))
+    )(*map(stay, (fields, order_rows, twiddle, y_high, y_low, order)))
     pieces = 2 * stack
     kept = pl.pallas_call(
         functools.partial(keep_kernel, 1.0 / math.sqrt(nx * ny)),

time: 193 us -> 190 us (0.984); the launches traced: 193 us -> 187 us
  Pallas kernels: 193 us -> 187 us
    pallas_call x1, Pallas kernels: 191 us -> 185 us  [kernel_shards(): pl.pallas_call(functools.partial(exchange_kernel, gx, gy, levels, chunks)...]
where the time goes in v2:
time: 190 us; the launch traced here: 187 us
  Pallas kernels  187 us (98%)
    pallas_call x1, Pallas kernels, kernel_shards(): pl.pallas_call(functools.partial(exchange_kernel, gx, gy, levels, chunks)...  185 us

profile of v2, /device:TPU:0, one launch (start us, length us, event | category | flops | bytes accessed | tf_op | source)
XLA Modules:
  0.0 187.3 jit_solution(12120201967460846857)
XLA Ops:
  0.0 0.0 copy-start
  0.0 185.1 %exchange.1 = f32[2,8,4,32,512]{4,3,2,1,0:T(8,128)S(1)} custom-call(f32[8,256,512]{2,1,0:T(8,128)} %fields.1, s32[8,128]{1,0:T(8,128)} %bitcast.4, f32[8,512]{1,0:T(8,128)} %constant.8.clone.twiddle_in, bf16[4,512,256]{2,1,0:T(8,128)(2,1)} %constant.9.clone.y_high_in, bf16[4,512,256]{2,1,0:T(8,128)(2,1)} %constant.10.clone.y_low_in, ...), custom_call_target="tpu_custom_call" | custom-call | tf_op jit(solution)/shard_map/exchange/pallas_call | solution.py:444
  185.2 0.0 copy-done
  185.2 2.2 %keep.1 = f32[16,128,512]{2,1,0:T(8,128)} custom-call(f32[16,128,512]{2,1,0:T(8,128)S(1)} %bitcast.3, s32[128,512]{1,0:T(8,128)S(1)} %copy-done), custom_call_target="tpu_custom_call" | custom-call | tf_op jit(solution)/shard_map/keep/pallas_call | solution.py:479
Async XLA Ops:
  0.0 185.2 %copy-start = (s32[128,512]{1,0:T(8,128)S(1)}, s32[128,512]{1,0:T(8,128)}, u32[]{:S(2)}) copy-start(s32[128,512]{1,0:T(8,128)} %kept_mask.1) | copy-start | bytes 786436

commit v3 on v2

--- a/solution.py
+++ b/solution.py
@@ -106,7 +106,7 @@
     fields, order_rows_in, twiddle_in, y_high_in, y_low_in, order_in, out,
     order_rows, twiddle, order_column, x_high, x_low, lines, split_lines, waves, held, columns, z_high, z_low, spectra,
     y_high, y_low, order, whole_y,
-    send_r, recv_r, send_a, recv_a, send_b, recv_b, send_c, recv_c, send_d, recv_d, table_sem,
+    send_r, recv_r, send_a, recv_a, send_b, recv_b, send_c, recv_c, send_d, recv_d, table_sem, go,
 ):
     me = lax.axis_index("gx")
     my = lax.axis_index("gy")
@@ -129,8 +129,14 @@
             total = total + bit * lax.rem(index // bit + o // bit, 2)
         return total
 
+    def inner_at(y_index):
+        return lax.rem(y_index + 1, gy) // 2
+
+    def lone_at(x_index, y_index):
+        return inner_at(y_index) * (1 - lax.rem(x_index + y_index, 2))
+
     def turn(step):
-        inner = lax.rem(my + 1, gy) // 2
+        inner = inner_at(my)
         is_first = (3 - step) // 3
         is_second = lax.rem(step, 2) * ((3 - step) // 2)
         is_third = step // 2 * ((4 - step) // 2)
@@ -335,14 +341,40 @@
         lax.fori_loop(0, gy, one, 0)
 
     barrier = pltpu.get_barrier_semaphore()
-    for axis, index, size in (("gy", my, gy), ("gx", me, gx)):
-        for o in range(1, size):
-            pl.semaphore_signal(
-                barrier, inc=1, device_id={axis: partner(index, o)}, device_id_type=MESH_IDS
+    lone = lone_at(me, my)
+
+    def greet(semaphore, axis, target):
+        pl.semaphore_signal(
+            semaphore, inc=1, device_id={axis: target}, device_id_type=MESH_IDS
+        )
+
+    greet(barrier, "gy", partner(my, gy - 1))
+    for o in range(1, gy - 1):
+        to = partner(my, o)
+        pl.when(lone_at(me, to) == 0)(functools.partial(greet, barrier, "gy", to))
+    for o in range(1, gx):
+        to = partner(me, o)
+        pl.when(lone_at(to, my) == 0)(functools.partial(greet, barrier, "gx", to))
+    pl.semaphore_wait(barrier, 1 + (1 - lone) * (gx + gy - 3))
+    start_all(copy_r, 0, (gy - 1,))
+
+    def release():
+        for o in range(1, gy - 1):
+            to = partner(my, o)
+            pl.when(lone_at(me, to) * (1 - inner_at(my)) == 1)(
+                functools.partial(greet, go, "gy", to)
             )
-    pl.semaphore_wait(barrier, gx + gy - 2)
-
-    start_all(copy_r, 0, y_order)
+        for o in range(1, gx):
+            to = partner(me, o)
+            pl.when(lone_at(to, my) == 1)(functools.partial(greet, go, "gx", to))
+        to = partner(my, gy - 1)
+        pl.when(lone_at(me, to) * (1 - inner_at(my)) == 1)(
+            functools.partial(greet, go, "gy", to)
+        )
+
+    pl.when(lone == 0)(release)
+    pl.when(lone == 1)(lambda: pl.semaphore_wait(go, gx // 2 + gy // 2))
+    start_all(copy_r, 0, y_order[1:])
     start_all(copy_a, 0, x_order)
     tables = [
         pltpu.make_async_copy(src, dst, table_sem.at[i])
@@ -469,7 +501,7 @@
         + [pltpu.SemaphoreType.DMA((chunks, gx))] * 2
         + [pltpu.SemaphoreType.DMA((2, chunks, gx))] * 2
         + [pltpu.SemaphoreType.DMA((chunks, gy))] * 4
-        + [pltpu.SemaphoreType.DMA((5,))],
+        + [pltpu.SemaphoreType.DMA((5,)), pltpu.SemaphoreType.REGULAR],
         compiler_params=pltpu.CompilerParams(
             collective_id=0, has_side_effects=True, vmem_limit_bytes=58 * 1024 * 1024
         ),

time: 190 us -> 189 us (level)
  the two profiles are of different devices: /device:TPU:0 before, /device:TPU:15 now
where the time goes in v3:
time: 189 us
  Pallas kernels  189 us (100%)
    pallas_call x1, Pallas kernels, kernel_shards(): pl.pallas_call(functools.partial(exchange_kernel, gx, gy, levels, chunks)...  187 us

profile of v3, /device:TPU:15, one launch (start us, length us, event | category | flops | bytes accessed | tf_op | source)
XLA Modules:
  0.0 188.8 jit_solution(7090563047057738358)
XLA Ops:
  0.0 0.0 copy-start
  0.0 186.6 %exchange.1 = f32[2,8,4,32,512]{4,3,2,1,0:T(8,128)S(1)} custom-call(f32[8,256,512]{2,1,0:T(8,128)} %fields.1, s32[8,128]{1,0:T(8,128)} %bitcast.4, f32[8,512]{1,0:T(8,128)} %constant.8.clone.twiddle_in, bf16[4,512,256]{2,1,0:T(8,128)(2,1)} %constant.9.clone.y_high_in, bf16[4,512,256]{2,1,0:T(8,128)(2,1)} %constant.10.clone.y_low_in, ...), custom_call_target="tpu_custom_call" | custom-call | tf_op jit(solution)/shard_map/exchange/pallas_call | solution.py:476
  186.6 0.0 copy-done
  186.6 2.2 %keep.1 = f32[16,128,512]{2,1,0:T(8,128)} custom-call(f32[16,128,512]{2,1,0:T(8,128)S(1)} %bitcast.3, s32[128,512]{1,0:T(8,128)S(1)} %copy-done), custom_call_target="tpu_custom_call" | custom-call | tf_op jit(solution)/shard_map/keep/pallas_call | solution.py:511
Async XLA Ops:
  0.0 186.6 %copy-start = (s32[128,512]{1,0:T(8,128)S(1)}, s32[128,512]{1,0:T(8,128)}, u32[]{:S(2)}) copy-start(s32[128,512]{1,0:T(8,128)} %kept_mask.1) | copy-start | bytes 786436

commit v4 on v3

--- a/solution.py
+++ b/solution.py
@@ -133,7 +133,7 @@
         return lax.rem(y_index + 1, gy) // 2
 
     def lone_at(x_index, y_index):
-        return inner_at(y_index) * (1 - lax.rem(x_index + y_index, 2))
+        return inner_at(y_index) * lax.rem(x_index, 2)
 
     def turn(step):
         inner = inner_at(my)
@@ -367,10 +367,6 @@
         for o in range(1, gx):
             to = partner(me, o)
             pl.when(lone_at(to, my) == 1)(functools.partial(greet, go, "gx", to))
-        to = partner(my, gy - 1)
-        pl.when(lone_at(me, to) * (1 - inner_at(my)) == 1)(
-            functools.partial(greet, go, "gy", to)
-        )
 
     pl.when(lone == 0)(release)
     pl.when(lone == 1)(lambda: pl.semaphore_wait(go, gx // 2 + gy // 2))

time: 189 us -> 187 us (0.989)
  the two profiles are of different devices: /device:TPU:15 before, /device:TPU:0 now
where the time goes in v4:
time: 187 us
  Pallas kernels  187 us (100%)
    pallas_call x1, Pallas kernels, kernel_shards(): pl.pallas_call(functools.partial(exchange_kernel, gx, gy, levels, chunks)...  185 us

profile of v4, /device:TPU:0, one launch (start us, length us, event | category | flops | bytes accessed | tf_op | source)
XLA Modules:
  0.0 186.9 jit_solution(2383923157218412489)
XLA Ops:
  0.0 0.0 copy-start
  0.0 184.7 %exchange.1 = f32[2,8,4,32,512]{4,3,2,1,0:T(8,128)S(1)} custom-call(f32[8,256,512]{2,1,0:T(8,128)} %fields.1, s32[8,128]{1,0:T(8,128)} %bitcast.4, f32[8,512]{1,0:T(8,128)} %constant.8.clone.twiddle_in, bf16[4,512,256]{2,1,0:T(8,128)(2,1)} %constant.9.clone.y_high_in, bf16[4,512,256]{2,1,0:T(8,128)(2,1)} %constant.10.clone.y_low_in, ...), custom_call_target="tpu_custom_call" | custom-call | tf_op jit(solution)/shard_map/exchange/pallas_call | solution.py:472
  184.7 0.0 copy-done
  184.7 2.2 %keep.1 = f32[16,128,512]{2,1,0:T(8,128)} custom-call(f32[16,128,512]{2,1,0:T(8,128)S(1)} %bitcast.3, s32[128,512]{1,0:T(8,128)S(1)} %copy-done), custom_call_target="tpu_custom_call" | custom-call | tf_op jit(solution)/shard_map/keep/pallas_call | solution.py:507
Async XLA Ops:
  0.0 184.7 %copy-start = (s32[128,512]{1,0:T(8,128)S(1)}, s32[128,512]{1,0:T(8,128)}, u32[]{:S(2)}) copy-start(s32[128,512]{1,0:T(8,128)} %kept_mask.1) | copy-start | bytes 786436

commit v5 on v4

--- a/solution.py
+++ b/solution.py
@@ -141,6 +141,8 @@
         is_second = lax.rem(step, 2) * ((3 - step) // 2)
         is_third = step // 2 * ((4 - step) // 2)
         return is_first * (1 + inner) + is_second * 3 + is_third * (2 - inner)
+
+    lone = lone_at(me, my)
 
     def move(axis, target, src, dst, send, recv):
         def remote():
@@ -334,15 +336,14 @@
             ordered = mxu(high, order[...]) + mxu(low, order[...])
             spectra[c, o] = ordered.reshape(2, levels, rows, y_local)
             remote, local = copy_d(c, o)
-            pl.when(o != 0)(lambda: remote().start())
+            now = lone * (o // 2) == 0 if c in (2, 3) else o >= 0
+            pl.when(jnp.logical_and(o != 0, now))(lambda: remote().start())
             pl.when(o == 0)(lambda: local().start())
             return carry
 
         lax.fori_loop(0, gy, one, 0)
 
     barrier = pltpu.get_barrier_semaphore()
-    lone = lone_at(me, my)
-
     def greet(semaphore, axis, target):
         pl.semaphore_signal(
             semaphore, inc=1, device_id={axis: target}, device_id_type=MESH_IDS
@@ -426,6 +427,16 @@
     y_stage(2)
     y_stage(3)
 
+    def yielding():
+        copy_d(1, 3)[0]().wait_send()
+        copy_d(2, 2)[0]().start()
+        copy_d(2, 2)[0]().wait_send()
+        copy_d(2, 3)[0]().start()
+        copy_d(3, 2)[0]().start()
+        copy_d(3, 3)[0]().start()
+
+    pl.when(lone == 1)(yielding)
+
     def sent(copy, c, offsets):
         for o in offsets:
             if o:
@@ -439,7 +450,11 @@
             sent(copy, c, x_order)
         if c < first:
             sent(copy_c, c, y_order)
-        sent(copy_d, c, y_order)
+        for o in (1, 2, 3):
+            if (c, o) in ((1, 3), (2, 2)):
+                pl.when(lone == 0)(copy_d(c, o)[0]().wait_send)
+            else:
+                sent(copy_d, c, (o,))
 
 
 def keep_kernel(scale, spectra, kept_mask, out, kept, sems):

time: 187 us -> 187 us (level)
  no operation moved by 1% of the time
where the time goes in v5:
time: 187 us
  Pallas kernels  187 us (100%)
    pallas_call x1, Pallas kernels, kernel_shards(): pl.pallas_call(functools.partial(exchange_kernel, gx, gy, levels, chunks)...  185 us

profile of v5, /device:TPU:0, one launch (start us, length us, event | category | flops | bytes accessed | tf_op | source)
XLA Modules:
  0.0 186.9 jit_solution(16331099736814697294)
XLA Ops:
  0.0 0.0 copy-start
  0.0 184.7 %exchange.1 = f32[2,8,4,32,512]{4,3,2,1,0:T(8,128)S(1)} custom-call(f32[8,256,512]{2,1,0:T(8,128)} %fields.1, s32[8,128]{1,0:T(8,128)} %bitcast.4, f32[8,512]{1,0:T(8,128)} %constant.8.clone.twiddle_in, bf16[4,512,256]{2,1,0:T(8,128)(2,1)} %constant.9.clone.y_high_in, bf16[4,512,256]{2,1,0:T(8,128)(2,1)} %constant.10.clone.y_low_in, ...), custom_call_target="tpu_custom_call" | custom-call | tf_op jit(solution)/shard_map/exchange/pallas_call | solution.py:487
  184.7 0.0 copy-done
  184.7 2.2 %keep.1 = f32[16,128,512]{2,1,0:T(8,128)} custom-call(f32[16,128,512]{2,1,0:T(8,128)S(1)} %bitcast.3, s32[128,512]{1,0:T(8,128)S(1)} %copy-done), custom_call_target="tpu_custom_call" | custom-call | tf_op jit(solution)/shard_map/keep/pallas_call | solution.py:522
Async XLA Ops:
  0.0 184.7 %copy-start = (s32[128,512]{1,0:T(8,128)S(1)}, s32[128,512]{1,0:T(8,128)}, u32[]{:S(2)}) copy-start(s32[128,512]{1,0:T(8,128)} %kept_mask.1) | copy-start | bytes 786436

commit v6 on v4

--- a/solution.py
+++ b/solution.py
@@ -104,9 +104,9 @@
 def exchange_kernel(
     gx, gy, levels, chunks,
     fields, order_rows_in, twiddle_in, y_high_in, y_low_in, order_in, out,
-    order_rows, twiddle, order_column, x_high, x_low, lines, split_lines, waves, held, columns, z_high, z_low, spectra,
+    staged, order_rows, twiddle, order_column, x_high, x_low, lines, split_lines, waves, held, columns, z_high, z_low, spectra,
     y_high, y_low, order, whole_y,
-    send_r, recv_r, send_a, recv_a, send_b, recv_b, send_c, recv_c, send_d, recv_d, table_sem, go,
+    send_r, recv_r, send_a, recv_a, send_b, recv_b, send_c, recv_c, send_d, recv_d, table_sem, stage_sem, go,
 ):
     me = lax.axis_index("gx")
     my = lax.axis_index("gy")
@@ -157,7 +157,8 @@
     def copy_r(c, o):
         to = partner(my, o)
         return move(
-            "gy", to, fields.at[first * levels + to], whole_y.at[my],
+            "gy", to, staged.at[o - 1] if o in (1, 2) else fields.at[first * levels + to],
+            whole_y.at[my],
             send_r.at[c, o], recv_r.at[c, o],
         )
 
@@ -357,6 +358,14 @@
         pl.when(lone_at(to, my) == 0)(functools.partial(greet, barrier, "gx", to))
     pl.semaphore_wait(barrier, 1 + (1 - lone) * (gx + gy - 3))
     start_all(copy_r, 0, (gy - 1,))
+    stages = [
+        pltpu.make_async_copy(
+            fields.at[first * levels + partner(my, o)], staged.at[o - 1], stage_sem.at[o - 1]
+        )
+        for o in (1, 2)
+    ]
+    for stage in stages:
+        stage.start()
 
     def release():
         for o in range(1, gy - 1):
@@ -370,6 +379,8 @@
 
     pl.when(lone == 0)(release)
     pl.when(lone == 1)(lambda: pl.semaphore_wait(go, gx // 2 + gy // 2))
+    for stage in stages:
+        stage.wait()
     start_all(copy_r, 0, y_order[1:])
     start_all(copy_a, 0, x_order)
     tables = [
@@ -475,6 +486,7 @@
         in_specs=[hbm] * 6,
         out_specs=anywhere,
         scratch_shapes=[
+            pltpu.VMEM((2, x_local, y_local), jnp.float32),
             pltpu.VMEM(order_rows.shape, jnp.int32),
             pltpu.VMEM(twiddle.shape, jnp.float32),
             pltpu.VMEM((wave_order.shape[0], LANES), jnp.int32),
@@ -497,7 +509,7 @@
         + [pltpu.SemaphoreType.DMA((chunks, gx))] * 2
         + [pltpu.SemaphoreType.DMA((2, chunks, gx))] * 2
         + [pltpu.SemaphoreType.DMA((chunks, gy))] * 4
-        + [pltpu.SemaphoreType.DMA((5,)), pltpu.SemaphoreType.REGULAR],
+        + [pltpu.SemaphoreType.DMA((5,)), pltpu.SemaphoreType.DMA((2,)), pltpu.SemaphoreType.REGULAR],
         compiler_params=pltpu.CompilerParams(
             collective_id=0, has_side_effects=True, vmem_limit_bytes=58 * 1024 * 1024
         ),

time: 187 us -> 187 us (level)
  no operation moved by 1% of the time
where the time goes in v6:
time: 187 us
  Pallas kernels  187 us (100%)
    pallas_call x1, Pallas kernels, kernel_shards(): pl.pallas_call(functools.partial(exchange_kernel, gx, gy, levels, chunks)...  185 us

profile of v6, /device:TPU:0, one launch (start us, length us, event | category | flops | bytes accessed | tf_op | source)
XLA Modules:
  0.0 186.9 jit_solution(14488654973065468576)
XLA Ops:
  0.0 0.0 copy-start
  0.0 184.7 %exchange.1 = f32[2,8,4,32,512]{4,3,2,1,0:T(8,128)S(1)} custom-call(f32[8,256,512]{2,1,0:T(8,128)} %fields.1, s32[8,128]{1,0:T(8,128)} %bitcast.4, f32[8,512]{1,0:T(8,128)} %constant.8.clone.twiddle_in, bf16[4,512,256]{2,1,0:T(8,128)(2,1)} %constant.9.clone.y_high_in, bf16[4,512,256]{2,1,0:T(8,128)(2,1)} %constant.10.clone.y_low_in, ...), custom_call_target="tpu_custom_call" | custom-call | tf_op jit(solution)/shard_map/exchange/pallas_call | solution.py:483
  184.7 0.0 copy-done
  184.7 2.2 %keep.1 = f32[16,128,512]{2,1,0:T(8,128)} custom-call(f32[16,128,512]{2,1,0:T(8,128)S(1)} %bitcast.3, s32[128,512]{1,0:T(8,128)S(1)} %copy-done), custom_call_target="tpu_custom_call" | custom-call | tf_op jit(solution)/shard_map/keep/pallas_call | solution.py:519
Async XLA Ops:
  0.0 184.7 %copy-start = (s32[128,512]{1,0:T(8,128)S(1)}, s32[128,512]{1,0:T(8,128)}, u32[]{:S(2)}) copy-start(s32[128,512]{1,0:T(8,128)} %kept_mask.1) | copy-start | bytes 786436
